TPU v7x, 32 devices: a whole 2x2x4 slice. The times are simulated.
32 devices in a mesh: rep: 2 (over x), shard: 16 (over z, y, core).
Axes of the slice: x: 2, y: 2, z: 4, core: 2. Of those that a mesh axis runs over, the one named last changes fastest.
Arguments:
- tokens: bfloat16 [4096, 2048], P(('rep', 'shard')), may hold values from -6 to 6
- segment_ids: int32 [4096], P(('rep', 'shard')), may hold values from -1 to 31, as said below
- cotangent: bfloat16 [4096, 2048], P(('rep', 'shard')), may hold values from -6 to 6
- w_qkv: bfloat16 [2048, 6144], P('shard'), may hold values from -0.125 to 0.125
- w_out: bfloat16 [2048, 2048], P('shard'), may hold values from -0.125 to 0.125
- w_gate_up: bfloat16 [2048, 16384], P('shard'), may hold values from -0.125 to 0.125
- w_down: bfloat16 [8192, 2048], P('shard'), may hold values from -0.0625 to 0.0625
- q_gain: bfloat16 [2048], P('shard'), may hold values from 0.5 to 1.5
- k_gain: bfloat16 [2048], P('shard'), may hold values from 0.5 to 1.5
- attn_gain: bfloat16 [2048], P('shard'), may hold values from 0.5 to 1.5
- mlp_gain: bfloat16 [2048], P('shard'), may hold values from 0.5 to 1.5
Outputs:
- output: bfloat16 [4096, 2048], P(('rep', 'shard'))
- grad_tokens: float32 [4096, 2048], P(('rep', 'shard'))
- grad_qkv: float32 [2048, 6144], P('shard')
- grad_out: float32 [2048, 2048], P('shard')
- grad_gate_up: float32 [2048, 16384], P('shard')
- grad_down: float32 [8192, 2048], P('shard')
- grad_q_gain: float32 [2048], P('shard')
- grad_k_gain: float32 [2048], P('shard')
- grad_attn_gain: float32 [2048], P('shard')
- grad_mlp_gain: float32 [2048], P('shard')
Inputs may be any that keep to these rules, and one draw needn't show every extreme that they name: `segment_ids`: within each block of 128 slots, live slots come first in runs of equal ids numbered upwards from 0 (one packed sequence each), each run starting at a slot whose index within the block is a multiple of 4, then padding slots with id -1; at least one block has no padding and starts a run at every multiple of 4.
All inputs are finite; a program needn't handle non-finite values.
Results may differ from a plain program's by a relative error of at most 0.02.
Values may be sent and summed in bfloat16 or wider, within the bound.
A program may use at most 384 MiB of HBM per device.

v0:
```python
import jax
import jax.numpy as jnp
from jax import lax
from jax.sharding import PartitionSpec as P

H = 16
EPSILON = 1e-06
THETA = 500000.0


def positions(seg_row):
    count = seg_row.shape[0]
    slots = jnp.arange(count, dtype=jnp.int32)
    starts = jnp.concatenate([jnp.ones((1,), jnp.bool_), seg_row[1:] != seg_row[:-1]])
    first = lax.cummax(jnp.where(starts, slots, 0), axis=0)
    return slots - first


def rope_tables(seg_row, head_width):
    half_width = head_width // 2
    spots = positions(seg_row).astype(jnp.float32)
    inverse = THETA ** (-(2.0 * jnp.arange(half_width, dtype=jnp.float32)) / head_width)
    angle = spots[:, None] * inverse[None, :]
    return (jnp.cos(angle), jnp.sin(angle))


def rotate(matrix, cosine, sine, num_heads):
    count, width = matrix.shape
    shaped = matrix.reshape(count, num_heads, width // num_heads)
    half_width = shaped.shape[2] // 2
    first_half = shaped[..., :half_width]
    second_half = shaped[..., half_width:]
    cos_head = cosine[:, None, :]
    sin_head = sine[:, None, :]
    joined = jnp.concatenate(
        [
            first_half * cos_head - second_half * sin_head,
            second_half * cos_head + first_half * sin_head,
        ],
        axis=-1,
    )
    return joined.reshape(count, width)


def allowed(seg_row):
    count = seg_row.shape[0]
    slots = jnp.arange(count)
    return (seg_row[:, None] == seg_row[None, :]) & (slots[None, :] <= slots[:, None])


def norm_forward(vector, gain):
    rscale = lax.rsqrt(jnp.mean(vector * vector, axis=-1, keepdims=True) + EPSILON)
    normed = vector * rscale
    return (normed * gain, normed, rscale)


def norm_backward(upstream, normed, rscale, gain):
    scaled = upstream * gain
    inner = jnp.mean(scaled * normed, axis=-1, keepdims=True)
    return (rscale * (scaled - normed * inner), jnp.sum(upstream * normed, axis=0))


def contract_last(left, right):
    return lax.dot_general(
        left, right, (((1,), (1,)), ((), ())), preferred_element_type=jnp.float32
    )


def contract_first(left, right):
    return lax.dot_general(
        left, right, (((0,), (0,)), ((), ())), preferred_element_type=jnp.float32
    )


def head_split(matrix, num_heads):
    return matrix.reshape(matrix.shape[0], num_heads, -1)


def attention_scores(query_rot, keys_rot, seg_row, num_heads):
    head_width = query_rot.shape[1] // num_heads
    scores = jnp.einsum(
        "thd,shd->hts",
        head_split(query_rot, num_heads),
        head_split(keys_rot, num_heads),
        preferred_element_type=jnp.float32,
    ) * head_width ** (-0.5)
    return jnp.where(allowed(seg_row)[None], scores, -1e30)


def attention_forward(query_rot, keys_rot, values_b, seg_row, num_heads):
    scores = attention_scores(query_rot, keys_rot, seg_row, num_heads)
    top = jnp.max(scores, axis=-1, keepdims=True)
    log_total = top[..., 0] + jnp.log(jnp.sum(jnp.exp(scores - top), axis=-1))
    probs_b = jnp.exp(scores - log_total[..., None]).astype(jnp.bfloat16)
    context = jnp.einsum(
        "hts,shd->thd", probs_b, head_split(values_b, num_heads), preferred_element_type=jnp.float32
    )
    return (context.reshape(query_rot.shape), log_total)


def attention_backward(
    query_rot, keys_rot, values_b, seg_row, log_total, context, d_context_b, num_heads
):
    count, width = query_rot.shape
    head_width = width // num_heads
    scores = attention_scores(query_rot, keys_rot, seg_row, num_heads)
    probs = jnp.exp(scores - log_total[..., None])
    probs_b = probs.astype(jnp.bfloat16)
    d_heads = head_split(d_context_b, num_heads)
    d_values = jnp.einsum("hts,thd->shd", probs_b, d_heads, preferred_element_type=jnp.float32)
    d_probs = jnp.einsum(
        "thd,shd->hts", d_heads, head_split(values_b, num_heads), preferred_element_type=jnp.float32
    )
    delta = jnp.sum(
        d_heads.astype(jnp.float32) * context.reshape(count, num_heads, head_width), axis=-1
    ).T
    d_scores_b = (probs * (d_probs - delta[..., None]) * head_width ** (-0.5)).astype(jnp.bfloat16)
    d_query = jnp.einsum(
        "hts,shd->thd",
        d_scores_b,
        head_split(keys_rot, num_heads),
        preferred_element_type=jnp.float32,
    )
    d_keys = jnp.einsum(
        "hts,thd->shd",
        d_scores_b,
        head_split(query_rot, num_heads),
        preferred_element_type=jnp.float32,
    )
    return (
        d_query.reshape(count, width),
        d_keys.reshape(count, width),
        d_values.reshape(count, width),
    )


def add_block(left, weight_rows):
    return jnp.dot(left, weight_rows, preferred_element_type=jnp.float32)


def fold_gain(left, pieces):
    weight_rows, gain_piece = pieces
    return (add_block(left, weight_rows), gain_piece)


def fold_two_gains(left, pieces):
    weight_rows, first_piece, second_piece = pieces
    return (add_block(left, weight_rows), first_piece, second_piece)


def back_rows(upstream, piece):
    return contract_last(upstream, piece)


def fold_owned(left_rows, upstream_piece):
    return contract_first(left_rows, upstream_piece)


def fold_all_owned(lefts, pieces):
    return tuple((fold_owned(left_rows, piece) for left_rows, piece in zip(lefts, pieces)))


def shards(
    tokens,
    segment_ids,
    cotangent,
    w_qkv,
    w_out,
    w_gate_up,
    w_down,
    q_gain,
    k_gain,
    attn_gain,
    mlp_gain,
):
    count, width = tokens.shape
    ff_width = w_gate_up.shape[1] // 2
    num_heads = H
    cosine, sine = rope_tables(segment_ids, width // num_heads)
    qkv, query_gain_full, keys_gain_full = fold_two_gains(
        tokens,
        (
            lax.all_gather(w_qkv, "shard", axis=0, tiled=True),
            lax.all_gather(q_gain, "shard", axis=0, tiled=True),
            lax.all_gather(k_gain, "shard", axis=0, tiled=True),
        ),
    )
    gain_query = query_gain_full.astype(jnp.float32)
    gain_keys = keys_gain_full.astype(jnp.float32)
    query_norm, query_hat, query_scale = norm_forward(qkv[:, :width], gain_query)
    keys_norm, keys_hat, keys_scale = norm_forward(qkv[:, width : 2 * width], gain_keys)
    query_rot = rotate(query_norm, cosine, sine, num_heads).astype(jnp.bfloat16)
    keys_rot = rotate(keys_norm, cosine, sine, num_heads).astype(jnp.bfloat16)
    values_b = qkv[:, 2 * width :].astype(jnp.bfloat16)
    context, log_total = attention_forward(query_rot, keys_rot, values_b, segment_ids, num_heads)
    context_b = context.astype(jnp.bfloat16)
    attn_raw, attn_gain_full = fold_gain(
        context_b,
        (
            lax.all_gather(w_out, "shard", axis=0, tiled=True),
            lax.all_gather(attn_gain, "shard", axis=0, tiled=True),
        ),
    )
    gain_attn = attn_gain_full.astype(jnp.float32)
    attn_norm, attn_hat, attn_scale = norm_forward(attn_raw, gain_attn)
    resid = tokens.astype(jnp.float32) + attn_norm
    resid_b = resid.astype(jnp.bfloat16)
    gate_up, mlp_gain_full = fold_gain(
        resid_b,
        (
            lax.all_gather(w_gate_up, "shard", axis=0, tiled=True),
            lax.all_gather(mlp_gain, "shard", axis=0, tiled=True),
        ),
    )
    gain_mlp = mlp_gain_full.astype(jnp.float32)
    gate_raw = gate_up[:, :ff_width]
    up_raw = gate_up[:, ff_width:]
    sigma = jax.nn.sigmoid(gate_raw)
    activated = gate_raw * sigma
    mixed_b = (activated * up_raw).astype(jnp.bfloat16)
    down_raw = add_block(mixed_b, lax.all_gather(w_down, "shard", axis=0, tiled=True))
    down_norm, down_hat, down_scale = norm_forward(down_raw, gain_mlp)
    output = (resid + down_norm).astype(jnp.bfloat16)
    valid = (segment_ids >= 0).astype(jnp.float32)[:, None]
    d_out = cotangent.astype(jnp.float32) * valid
    d_down, grad_mlp = norm_backward(d_out, down_hat, down_scale, gain_mlp)
    d_down_b = d_down.astype(jnp.bfloat16)
    d_mixed = back_rows(d_down_b, lax.all_gather(w_down, "shard", axis=0, tiled=True))
    d_gate = d_mixed * up_raw * sigma * (1.0 + gate_raw * (1.0 - sigma))
    d_up = d_mixed * activated
    d_gu_b = jnp.concatenate([d_gate, d_up], axis=1).astype(jnp.bfloat16)
    d_resid = d_out + back_rows(d_gu_b, lax.all_gather(w_gate_up, "shard", axis=0, tiled=True))
    d_attn, grad_attn = norm_backward(d_resid, attn_hat, attn_scale, gain_attn)
    d_attn_b = d_attn.astype(jnp.bfloat16)
    out_full, qkv_full = (
        lax.all_gather(w_out, "shard", axis=0, tiled=True),
        lax.all_gather(w_qkv, "shard", axis=0, tiled=True),
    )
    d_context_b = contract_last(d_attn_b, out_full).astype(jnp.bfloat16)
    d_query_rot, d_keys_rot, d_values = attention_backward(
        query_rot, keys_rot, values_b, segment_ids, log_total, context, d_context_b, num_heads
    )
    d_query_norm = rotate(d_query_rot, cosine, -sine, num_heads)
    d_keys_norm = rotate(d_keys_rot, cosine, -sine, num_heads)
    d_query, grad_query = norm_backward(d_query_norm, query_hat, query_scale, gain_query)
    d_keys, grad_keys = norm_backward(d_keys_norm, keys_hat, keys_scale, gain_keys)
    d_qkv_b = jnp.concatenate([d_query, d_keys, d_values], axis=1).astype(jnp.bfloat16)
    grad_tokens = d_resid + contract_last(d_qkv_b, qkv_full)
    mixed_rows, resid_rows, token_rows, context_rows = (
        lax.all_to_all(mixed_b, "shard", split_axis=1, concat_axis=0, tiled=True),
        lax.all_to_all(resid_b, "shard", split_axis=1, concat_axis=0, tiled=True),
        lax.all_to_all(tokens, "shard", split_axis=1, concat_axis=0, tiled=True),
        lax.all_to_all(context_b, "shard", split_axis=1, concat_axis=0, tiled=True),
    )
    grad_down, grad_gate_up, grad_qkv_own, grad_out_own = fold_all_owned(
        (mixed_rows, resid_rows, token_rows, context_rows),
        (
            lax.all_gather(d_down_b, "shard", axis=0, tiled=True),
            lax.all_gather(d_gu_b, "shard", axis=0, tiled=True),
            lax.all_gather(d_qkv_b, "shard", axis=0, tiled=True),
            lax.all_gather(d_attn_b, "shard", axis=0, tiled=True),
        ),
    )
    gains_own = (
        lax.psum_scatter(
            grad_query.astype(jnp.bfloat16), "shard", scatter_dimension=0, tiled=True
        ).astype(jnp.float32),
        lax.psum_scatter(
            grad_keys.astype(jnp.bfloat16), "shard", scatter_dimension=0, tiled=True
        ).astype(jnp.float32),
        lax.psum_scatter(
            grad_attn.astype(jnp.bfloat16), "shard", scatter_dimension=0, tiled=True
        ).astype(jnp.float32),
        lax.psum_scatter(
            grad_mlp.astype(jnp.bfloat16), "shard", scatter_dimension=0, tiled=True
        ).astype(jnp.float32),
    )
    summed = (
        lax.psum(grad_qkv_own.astype(jnp.bfloat16), "rep").astype(jnp.float32),
        lax.psum(grad_out_own.astype(jnp.bfloat16), "rep").astype(jnp.float32),
        lax.psum(grad_gate_up.astype(jnp.bfloat16), "rep").astype(jnp.float32),
        lax.psum(grad_down.astype(jnp.bfloat16), "rep").astype(jnp.float32),
        lax.psum(gains_own[0].astype(jnp.bfloat16), "rep").astype(jnp.float32),
        lax.psum(gains_own[1].astype(jnp.bfloat16), "rep").astype(jnp.float32),
        lax.psum(gains_own[2].astype(jnp.bfloat16), "rep").astype(jnp.float32),
        lax.psum(gains_own[3].astype(jnp.bfloat16), "rep").astype(jnp.float32),
    )
    grad_qkv, grad_out, grad_gu, grad_dn, grad_q, grad_k, grad_a, grad_m = summed
    return (
        output,
        grad_tokens,
        grad_qkv,
        grad_out,
        grad_gu,
        grad_dn,
        grad_q,
        grad_k,
        grad_a,
        grad_m,
    )


def solution(mesh):
    return jax.shard_map(
        shards,
        mesh=mesh,
        in_specs=(
            P(("rep", "shard"), None),
            P(("rep", "shard")),
            P(("rep", "shard"), None),
            P("shard", None),
            P("shard", None),
            P("shard", None),
            P("shard", None),
            P("shard"),
            P("shard"),
            P("shard"),
            P("shard"),
        ),
        out_specs=(
            P(("rep", "shard"), None),
            P(("rep", "shard"), None),
            P("shard", None),
            P("shard", None),
            P("shard", None),
            P("shard", None),
            P("shard"),
            P("shard"),
            P("shard"),
            P("shard"),
        ),
        check_vma=False,
    )
```

profile of v0, /device:TPU:0, one launch (start us, length us, event | category | flops | bytes accessed | tf_op | source)
XLA Modules:
  0.0 1692.7 jit_solution(17944830758551619071)
XLA Ops:
  10.1 23.4 %all-gather = bf16[16,1,128]{2,1,0:T(2,128)(2,1)S(1)} all-gather(bf16[1,1,128]{2,1,0:T(2,128)(2,1)S(1)} %bitcast.143), channel_id=1, replica_groups=mesh['rep'=2,'shard'=16] {'shard'}, dimensions={0}, use_global_device_ids=true | all-gather | bytes 4352 | tf_op jit(solution)/shard_map/all_gather | solution.py:184
  33.5 18.0 %all-gather.1 = bf16[16,1,128]{2,1,0:T(2,128)(2,1)S(1)} all-gather(bf16[1,1,128]{2,1,0:T(2,128)(2,1)S(1)} %bitcast.144), channel_id=1, replica_groups=mesh['rep'=2,'shard'=16] {'shard'}, dimensions={0}, use_global_device_ids=true | all-gather | bytes 4352 | tf_op jit(solution)/shard_map/all_gather | solution.py:185
  51.8 19.3 %all-gather.2 = bf16[16,1,128]{2,1,0:T(2,128)(2,1)S(1)} all-gather(bf16[1,1,128]{2,1,0:T(2,128)(2,1)S(1)} %bitcast.145), channel_id=1, replica_groups=mesh['rep'=2,'shard'=16] {'shard'}, dimensions={0}, use_global_device_ids=true | all-gather | bytes 4352 | tf_op jit(solution)/shard_map/all_gather | solution.py:201
  71.2 18.0 %all-gather.3 = bf16[16,1,128]{2,1,0:T(2,128)(2,1)S(1)} all-gather(bf16[1,1,128]{2,1,0:T(2,128)(2,1)S(1)} %bitcast.146), channel_id=1, replica_groups=mesh['rep'=2,'shard'=16] {'shard'}, dimensions={0}, use_global_device_ids=true | all-gather | bytes 4352 | tf_op jit(solution)/shard_map/all_gather | solution.py:212
  89.9 51.1 %all-gather.13.cloned.1.call-done = bf16[2048,6144]{1,0:T(8,128)(2,1)} async-done(((bf16[128,6144]{1,0:T(8,128)(2,1)}), bf16[2048,6144]{1,0:T(8,128)(2,1)}) %all-gather.13.cloned.1.call-update) | async-done | bytes 25165840 | tf_op jit(solution)/shard_map/all_gather | solution.py:183
  141.0 10.1 fusion.27
  152.7 1.4 subtract_convert_fusion.1
  156.7 1.5 fusion.26
  158.2 59.4 %all-gather.15.cloned.1.call-done = bf16[2048,2048]{1,0:T(8,128)(2,1)} async-done(((bf16[128,2048]{1,0:T(8,128)(2,1)}), bf16[2048,2048]{1,0:T(8,128)(2,1)}) %all-gather.15.cloned.1.call-update) | async-done | bytes 8388624 | tf_op jit(solution)/shard_map/all_gather | solution.py:200
  217.7 5.0 multiply_reduce_fusion.8
  224.6 319.3 %all-gather.17.cloned.1.call-done = bf16[2048,16384]{1,0:T(8,128)(2,1)} async-done(((bf16[128,16384]{1,0:T(8,128)(2,1)}), bf16[2048,16384]{1,0:T(8,128)(2,1)}) %all-gather.17.cloned.1.call-update) | async-done | bytes 67108880 | tf_op jit(solution)/shard_map/all_gather | solution.py:211
  544.0 29.4 %fusion.28 = f32[128,16384]{1,0:T(8,128)} fusion(bf16[128,2048]{1,0:T(8,128)(2,1)} %fusion.10, bf16[2048,16384]{1,0:T(8,128)(2,1)} %all-gather.17.cloned.1.call-done), kind=kOutput, calls=%fused_computation.105 | convolution fusion | flops 8589934592 | bytes 76021760 | tf_op jit(solution)/shard_map/dot_general | solution.py:138
  573.3 6.0 multiply_convert_fusion.2
  579.3 134.2 %all-gather.19.cloned.1.call-done = bf16[8192,2048]{1,0:T(8,128)(2,1)} async-done(((bf16[512,2048]{1,0:T(8,128)(2,1)}), bf16[8192,2048]{1,0:T(8,128)(2,1)}) %all-gather.19.cloned.1.call-update) | async-done | bytes 33554448 | tf_op jit(solution)/shard_map/all_gather | solution.py:221
  713.5 13.6 multiply_reduce_fusion.7
  728.1 1.2 multiply_convert_fusion.6
  729.3 20.1 %multiply_convert_fusion.1 = (bf16[128,8192]{1,0:T(8,128)(2,1)}, bf16[128,8192]{1,0:T(8,128)(2,1)}) fusion(f32[128,16384]{1,0:T(8,128)} %fusion.28, bf16[128,2048]{1,0:T(8,128)(2,1)} %multiply_convert_fusion.6, bf16[8192,2048]{1,0:T(8,128)(2,1)} %all-gather.19.cloned.1.call-done), kind=kOutput, calls=%fused_computation.5 | convolution fusion | flops 4308598784 | bytes 46661632 | tf_op jit(solution)/shard_map/dot_general | solution.py:64
  749.4 30.4 %multiply_reduce_fusion.1 = (bf16[2048]{0:T(1024)(128)(2,1)S(1)}, f32[128]{0:T(128)S(1)}, f32[128,2048]{1,0:T(8,128)}) fusion(f32[128,2048]{1,0:T(8,128)} %copy-done.2, f32[128]{0:T(128)S(1)} %add_rsqrt_fusion.1, f32[2048]{0:T(1024)S(1)} %bitcast.131, bf16[2048,16384]{1,0:T(8,128)(2,1)} %all-gather.17.cloned.1.call-done, ...), kind=kOutput, calls=%fused_computation.36 | convolution fusion | flops 8600680448 | bytes 73938432 | tf_op jit(solution)/shard_map/dot_general | solution.py:64
  779.8 3.4 multiply_convert_fusion.5
  784.1 7.3 convolution_convert_fusion.4
  791.3 2.1 copy.102
  793.4 2.7 convolution_convert_fusion.5
  796.0 2.0 copy.132
  798.1 1.6 multiply_reduce_fusion.4
  799.7 1.8 fusion.5
  806.4 1.2 pad_maximum_fusion.1
  807.7 3.9 pad_maximum_fusion
  813.0 27.7 %all_to_all.73 = bf16[128,16,128]{0,2,1:T(8,128)(2,1)} all-to-all(bf16[128,16,128]{0,2,1:T(8,128)(2,1)S(1)} %bitcast.127), channel_id=1, replica_groups=mesh['rep'=2,'shard'=16] {'shard'}, dimensions={1} | all-to-all | bytes 1048576 | tf_op jit(solution)/shard_map/all_to_all | solution.py:252
  840.6 9.8 all-to-all-start.1
  850.4 1.5 copy.170
  852.0 20.5 %all-to-all-done.1 = bf16[128,16,128]{0,2,1:T(8,128)(2,1)S(1)} async-done(((bf16[128,16,128]{0,2,1:T(8,128)(2,1)}), bf16[128,16,128]{0,2,1:T(8,128)(2,1)S(1)}, u32[]{:S(2)}, u32[]{:S(2)}) %all-to-all-start.1) | async-done | bytes 524320 | tf_op jit(solution)/shard_map/all_to_all | solution.py:253
  872.5 6.0 all-to-all-start.3
  880.1 5.5 convolution_convert_fusion.3
  885.5 50.8 %all-to-all-done.3 = bf16[128,16,512]{2,0,1:T(8,128)(2,1)} async-done(((bf16[128,16,512]{2,0,1:T(8,128)(2,1)}), bf16[128,16,512]{2,0,1:T(8,128)(2,1)}, u32[]{:S(2)}, u32[]{:S(2)}) %all-to-all-start.3) | async-done | bytes 2097184 | tf_op jit(solution)/shard_map/all_to_all | solution.py:250
  936.3 19.3 %all-to-all-start.2 = ((bf16[128,16,128]{2,0,1:T(8,128)(2,1)}), bf16[128,16,128]{2,0,1:T(8,128)(2,1)S(1)}, u32[]{:S(2)}, u32[]{:S(2)}) async-start(bf16[128,16,128]{2,0,1:T(8,128)(2,1)} %copy_bitcast_fusion.1), calls=%async_computation.2 | async-start | bytes 1048576 | tf_op jit(solution)/shard_map/all_to_all | solution.py:251
  956.1 35.1 %all-gather.27.cloned.1.call-done = bf16[2048,2048]{1,0:T(8,128)(2,1)} async-done(((bf16[128,2048]{1,0:T(8,128)(2,1)}), bf16[2048,2048]{1,0:T(8,128)(2,1)}) %all-gather.27.cloned.1.call-update) | async-done | bytes 8388624 | tf_op jit(solution)/shard_map/all_gather | solution.py:258
  991.2 9.9 convolution_convert_fusion.2
  1001.1 119.8 %all-gather.21.cloned.1.call-done = bf16[2048,6144]{1,0:T(8,128)(2,1)} async-done(((bf16[128,6144]{1,0:T(8,128)(2,1)}), bf16[2048,6144]{1,0:T(8,128)(2,1)}) %all-gather.21.cloned.1.call-update) | async-done | bytes 25165840 | tf_op jit(solution)/shard_map/all_gather | solution.py:260
  1120.9 12.9 fusion
  1133.8 315.4 %all-gather.25.cloned.1.call-done = bf16[2048,16384]{1,0:T(8,128)(2,1)} async-done(((bf16[128,16384]{1,0:T(8,128)(2,1)}), bf16[2048,16384]{1,0:T(8,128)(2,1)}) %all-gather.25.cloned.1.call-update) | async-done | bytes 67108880 | tf_op jit(solution)/shard_map/all_gather | solution.py:259
  1449.2 26.2 %convolution_convert_fusion = bf16[128,16384]{1,0:T(8,128)(2,1)} fusion(bf16[2048,128]{1,0:T(8,128)(2,1)S(1)} %bitcast.124, bf16[2048,16384]{1,0:T(8,128)(2,1)} %all-gather.25.cloned.1.call-done), kind=kOutput, calls=%fused_computation | convolution fusion | flops 8592031744 | bytes 71827456 | tf_op jit(solution)/shard_map/dot_general | solution.py:70
  1477.2 60.7 %all-reduce.4 = (bf16[2048]{0:T(1024)(128)(2,1)S(1)}, bf16[2048]{0:T(1024)(128)(2,1)S(1)}, bf16[2048]{0:T(1024)(128)(2,1)S(1)}, bf16[2048]{0:T(1024)(128)(2,1)S(1)}) all-reduce(bf16[2048]{0:T(1024)(128)(2,1)S(1)} %get-tuple-element.55, ...), channel_id=2, replica_groups=mesh['rep'=2,'shard'=16] {'shard'}, use_global_device_ids=true, to_apply=%region_17.18.clone | all-reduce | flops 8192 | bytes 32768
  1538.2 5.3 all-reduce.5
  1545.6 14.4 convolution_add_fusion
  1560.0 113.7 %all-reduce.9.cloned.1.call-done = (bf16[128,6144]{0,1:T(8,128)(2,1)}, bf16[128,2048]{1,0:T(8,128)(2,1)}, bf16[128,16384]{1,0:T(8,128)(2,1)}, bf16[512,2048]{1,0:T(8,128)(2,1)}) async-done(((bf16[128,6144]{0,1:T(8,128)(2,1)}, bf16[128,2048]{1,0:T(8,128)(2,1)}, bf16[128,16384]{1,0:T(8,128)(2,1)}, bf16[512,2048]{1,0:T(8,128)(2,1)}), (bf16[128,6144]{0,1:T(8,128)(2,1)}, bf16[128,2048]{1,0:T(8,128)(2,1)}, ...) | async-done | bytes 8388624 | tf_op jit(solution)/shard_map/psum | solution.py:279
  1673.7 6.6 convert_element_type.154
  1680.3 2.5 convert_element_type.156
  1682.8 2.1 copy.121
  (139 shorter events, 24.4 us)
Async XLA Ops:
  7.2 2.9 copy-start.29
  7.2 26.3 %copy-start.30 = (bf16[128]{0:T(256)(128)(2,1)S(1)}, bf16[128]{0:T(256)(128)(2,1)}, u32[]{:S(2)}) copy-start(bf16[128]{0:T(256)(128)(2,1)} %param.19) | copy-start | bytes 772
  7.2 44.3 %copy-start.28 = (s32[128]{0:T(128)S(1)}, s32[128]{0:T(128)}, u32[]{:S(2)}) copy-start(s32[128]{0:T(128)} %param.12) | copy-start | bytes 1540
  7.2 44.6 %copy-start.31 = (bf16[128]{0:T(256)(128)(2,1)S(1)}, bf16[128]{0:T(256)(128)(2,1)}, u32[]{:S(2)}) copy-start(bf16[128]{0:T(256)(128)(2,1)} %param.20) | copy-start | bytes 772
  7.2 63.9 %copy-start.32 = (bf16[128]{0:T(256)(128)(2,1)S(1)}, bf16[128]{0:T(256)(128)(2,1)}, u32[]{:S(2)}) copy-start(bf16[128]{0:T(256)(128)(2,1)} %param.21) | copy-start | bytes 772
  7.2 133.8 %all-gather.13.cloned.1.call-start = ((), (), s32[]{:S(2)}) async-start(), calls=%async_computation.4 | async-start | bytes 26738688 | tf_op jit(solution)/shard_map/all_gather | solution.py:183
  8.0 209.7 %all-gather.15.cloned.1.call-start = ((), (), s32[]{:S(2)}) async-start(), calls=%async_computation.5 | async-start | bytes 8912896 | tf_op jit(solution)/shard_map/all_gather | solution.py:200
  8.7 535.2 %all-gather.17.cloned.1.call-start = ((), (), s32[]{:S(2)}) async-start(), calls=%async_computation.6 | async-start | bytes 71303168 | tf_op jit(solution)/shard_map/all_gather | solution.py:211
  9.4 704.0 %all-gather.19.cloned.1.call-start = ((), (), s32[]{:S(2)}) async-start(), calls=%async_computation.7 | async-start | bytes 35651584 | tf_op jit(solution)/shard_map/all_gather | solution.py:221
  10.0 870.1 %all-gather.23.cloned.1.call-start = ((), (), s32[]{:S(2)}) async-start(), calls=%async_computation.9 | async-start | bytes 8912896 | tf_op jit(solution)/shard_map/all_gather | solution.py:261
  154.1 0.8 copy-start.9
  154.1 1.6 copy-start.11
  154.1 1.6 copy-start.13
  154.1 1.6 copy-start.15
  155.7 1.0 copy-start
  217.7 5.9 copy-start.4
  222.6 1.0 copy-start.2
  713.5 13.7 copy-start.8
  727.1 1.0 copy-start.3
  783.2 207.9 %all-gather.27.cloned.1.call-start = ((), (), s32[]{:S(2)}) async-start(), calls=%async_computation.11 | async-start | bytes 8912896 | tf_op jit(solution)/shard_map/all_gather | solution.py:258
  783.8 337.1 %all-gather.21.cloned.1.call-start = ((), (), s32[]{:S(2)}) async-start(), calls=%async_computation.8 | async-start | bytes 26738688 | tf_op jit(solution)/shard_map/all_gather | solution.py:260
  798.1 3.4 copy-start.14
  798.1 3.4 copy-start.16
  798.1 3.9 copy-start.10
  798.1 3.9 copy-start.12
  804.4 1.9 copy-start.20
  805.4 0.8 copy-start.22
  805.4 1.0 copy-start.24
  805.4 2.3 copy-start.6
  807.7 641.5 %all-gather.25.cloned.1.call-start = ((), (), s32[]{:S(2)}) async-start(), calls=%async_computation.10 | async-start | bytes 71303168 | tf_op jit(solution)/shard_map/all_gather | solution.py:259
  811.6 1.0 copy-start.5
  811.6 38.8 %copy-start.1 = (bf16[128,8192]{1,0:T(8,128)(2,1)S(1)}, bf16[128,8192]{1,0:T(8,128)(2,1)}, u32[]{:S(2)}) copy-start(bf16[128,8192]{1,0:T(8,128)(2,1)} %multiply_convert_fusion.2) | copy-start | bytes 6291460
  840.6 31.9 %all-to-all-start.1 = ((bf16[128,16,128]{0,2,1:T(8,128)(2,1)}), bf16[128,16,128]{0,2,1:T(8,128)(2,1)S(1)}, u32[]{:S(2)}, u32[]{:S(2)}) async-start(bf16[128,16,128]{0,2,1:T(8,128)(2,1)} %get-tuple-element.103), calls=%async_computation.1 | async-start | bytes 1048576 | tf_op jit(solution)/shard_map/all_to_all | solution.py:253
  850.4 28.4 %copy-start.7 = (bf16[128,2048]{1,0:T(8,128)(2,1)S(1)}, bf16[128,2048]{1,0:T(8,128)(2,1)}, u32[]{:S(2)}) copy-start(bf16[128,2048]{1,0:T(8,128)(2,1)} %fusion.10) | copy-start | bytes 1572868
  852.0 26.5 %copy-start.19 = (bf16[128,16,128]{0,2,1:T(8,128)(2,1)S(1)}, bf16[128,16,128]{0,2,1:T(8,128)(2,1)}, u32[]{:S(2)}) copy-start(bf16[128,16,128]{0,2,1:T(8,128)(2,1)} %all_to_all.73) | copy-start | bytes 1572868
  872.5 63.9 %all-to-all-start.3 = ((bf16[128,16,512]{2,0,1:T(8,128)(2,1)}), bf16[128,16,512]{2,0,1:T(8,128)(2,1)}, u32[]{:S(2)}, u32[]{:S(2)}) async-start(bf16[128,16,512]{2,0,1:T(8,128)(2,1)} %bitcast.120), calls=%async_computation.3 | async-start | bytes 4194304 | tf_op jit(solution)/shard_map/all_to_all | solution.py:250
  936.3 197.5 %all-to-all-start.2 = ((bf16[128,16,128]{2,0,1:T(8,128)(2,1)}), bf16[128,16,128]{2,0,1:T(8,128)(2,1)S(1)}, u32[]{:S(2)}, u32[]{:S(2)}) async-start(bf16[128,16,128]{2,0,1:T(8,128)(2,1)} %copy_bitcast_fusion.1), calls=%async_computation.2 | async-start | bytes 1048576 | tf_op jit(solution)/shard_map/all_to_all | solution.py:251
  955.7 718.0 %all-reduce.9.cloned.1.call-start = ((), (), s32[]{:S(2)}) async-start(), calls=%async_computation.12 | async-start | bytes 16777216 | tf_op jit(solution)/shard_map/psum | solution.py:279
  1475.3 0.7 copy-start.33
  1475.3 70.2 %copy-start.17 = (f32[128,2048]{1,0:T(8,128)S(1)}, f32[128,2048]{1,0:T(8,128)}, u32[]{:S(2)}) copy-start(f32[128,2048]{1,0:T(8,128)} %get-tuple-element.109) | copy-start | bytes 3145732
  1475.3 70.2 %copy-start.21 = (bf16[128,2048]{1,0:T(8,128)(2,1)S(1)}, bf16[128,2048]{1,0:T(8,128)(2,1)}, u32[]{:S(2)}) copy-start(bf16[128,2048]{1,0:T(8,128)(2,1)} %copy.132) | copy-start | bytes 1572868
  1475.3 70.2 %copy-start.23 = (bf16[128,2048]{1,0:T(8,128)(2,1)S(1)}, bf16[128,2048]{1,0:T(8,128)(2,1)}, u32[]{:S(2)}) copy-start(bf16[128,2048]{1,0:T(8,128)(2,1)} %copy-done.22) | copy-start | bytes 1572868
  1475.4 70.2 %copy-start.25 = (bf16[128,2048]{1,0:T(8,128)(2,1)S(1)}, bf16[128,2048]{1,0:T(8,128)(2,1)}, u32[]{:S(2)}) copy-start(bf16[128,2048]{1,0:T(8,128)(2,1)} %copy-done.24) | copy-start | bytes 1572868
  1673.7 6.6 copy-start.18
  1680.3 2.5 copy-start.26
  1680.3 4.6 copy-start.27
Sparse Core Ops, SparseCore 0:
  9.6 131.3 all-gather.12
  143.2 74.4 all-gather.14
  219.3 324.6 all-gather.16
  545.4 168.0 all-gather.18
  783.3 94.6 all-gather.22
  880.1 111.0 all-gather.26
  993.3 127.5 all-gather.20
  1123.1 326.0 all-gather.24
  1475.5 198.1 all-reduce.8
where the time goes:
time: 1700 us; the launch traced here: 1690 us
  waiting for transfers between devices  1220 us (72%)
  matrix products  192 us (11%)
  blocking collectives  172 us (10%)
  other arithmetic  36.9 us (2%)
  starting transfers between devices  36.1 us (2%)
  local copies, waits for them, and re-layouts  17.3 us (1%)
    all_gather x1, waiting for transfers between devices, shards(): lax.all_gather(w_gate_up, 'shard', axis=0, tiled=True)  319 us
    all_gather x1, waiting for transfers between devices, shards(): lax.all_gather(d_gu_b, 'shard', axis=0, tiled=True)  315 us
    all_gather x1, waiting for transfers between devices, shards(): lax.all_gather(w_down, 'shard', axis=0, tiled=True)  134 us
    all_gather x1, waiting for transfers between devices, shards(): lax.all_gather(d_qkv_b, 'shard', axis=0, tiled=True)  120 us
    psum x1, waiting for transfers between devices, shards(): lax.psum(grad_qkv_own.astype(jnp.bfloat16), 'rep').astype(jnp.float32)  114 us
    dot_general x4, matrix products, contract_last(): lax.dot_general(left, right, (((1,), (1,)), ((), ())), preferred_element_...  72.1 us
    unnamed x1, blocking collectives  60.7 us
    all_gather x1, waiting for transfers between devices, shards(): lax.all_gather(w_out, 'shard', axis=0, tiled=True)  59.4 us
  transfers between devices with their start and end apart: 12, of which 10 were waited for; matrix products, arithmetic and copies ran while one was open for 8% of the time, Pallas kernels for 0%

commit v1 on v0

--- a/solution.py
+++ b/solution.py
@@ -6,6 +6,27 @@
 H = 16
 EPSILON = 1e-06
 THETA = 500000.0
+
+
+def collect(x, axis, dim):
+    length, position, width = (lax.axis_size(axis), lax.axis_index(axis), x.shape[dim])
+    right = [(i, (i + 1) % length) for i in range(length)]
+    downward = [(i, (i - 1) % length) for i in range(length)]
+    out = jnp.zeros((*x.shape[:dim], length * width, *x.shape[dim + 1 :]), x.dtype)
+    out = lax.dynamic_update_slice_in_dim(out, x, position * width, axis=dim)
+    from_left = from_right = x
+    half = length // 2
+    for lap in range(1, half + 1):
+        from_left = lax.ppermute(from_left, axis, right)
+        out = lax.dynamic_update_slice_in_dim(
+            out, from_left, (position - lap) % length * width, axis=dim
+        )
+        if lap < length - half:
+            from_right = lax.ppermute(from_right, axis, downward)
+            out = lax.dynamic_update_slice_in_dim(
+                out, from_right, (position + lap) % length * width, axis=dim
+            )
+    return out
 
 
 def positions(seg_row):
@@ -207,10 +228,7 @@
     resid_b = resid.astype(jnp.bfloat16)
     gate_up, mlp_gain_full = fold_gain(
         resid_b,
-        (
-            lax.all_gather(w_gate_up, "shard", axis=0, tiled=True),
-            lax.all_gather(mlp_gain, "shard", axis=0, tiled=True),
-        ),
+        (collect(w_gate_up, "shard", 0), lax.all_gather(mlp_gain, "shard", axis=0, tiled=True)),
     )
     gain_mlp = mlp_gain_full.astype(jnp.float32)
     gate_raw = gate_up[:, :ff_width]

time: 1700 us -> 2320 us (1.36)
  starting transfers between devices: 36.1 us -> 603 us
  waiting for transfers between devices: 1220 us -> 1040 us
  blocking collectives: 172 us -> 329 us
  local copies, waits for them, and re-layouts: 17.3 us -> 94 us
    ppermute x0 -> x15, starting transfers between devices: none -> 572 us  [the longest x8 562 us: collect(): from_left = lax.ppermute(from_left, axis, right)]
    ppermute x0 -> x15, waiting for transfers between devices: none -> 432 us  [the longest x8 366 us: collect(): from_left = lax.ppermute(from_left, axis, right)]
    all_gather x1, waiting for transfers between devices: 319 us -> 0.01 us  [shards(): lax.all_gather(w_gate_up, 'shard', axis=0, tiled=True)]
    all_gather x1, waiting for transfers between devices: 134 us -> 0.01 us  [shards(): lax.all_gather(w_down, 'shard', axis=0, tiled=True)]
    all_gather x1, blocking collectives: 23.4 us -> 145 us  [shards(): lax.all_gather(q_gain, 'shard', axis=0, tiled=True)]
    all_gather x1, waiting for transfers between devices: 59.4 us -> 0.01 us  [shards(): lax.all_gather(w_out, 'shard', axis=0, tiled=True)]
    dynamic_update_slice x0 -> x16, local copies, waits for them, and re-layouts: none -> 53 us  [the longest x8 27.6 us: collect(): lax.dynamic_update_slice_in_dim(out, from_left, (position - lap) % length...]
    all_gather x1, waiting for transfers between devices: 51.1 us -> 0.01 us  [shards(): lax.all_gather(w_qkv, 'shard', axis=0, tiled=True)]
  transfers between devices with their start and end apart: 12 -> 27, of which waited for: 10 -> 12; matrix products, arithmetic and copies ran while one was open for 8% -> 12% of each run, Pallas kernels for 0% -> 0%
where the time goes in v1:
time: 2320 us
  waiting for transfers between devices  1040 us (45%)
  starting transfers between devices  603 us (26%)
  blocking collectives  329 us (14%)
  matrix products  193 us (8%)
  local copies, waits for them, and re-layouts  94 us (4%)
  other arithmetic  37 us (2%)
    ppermute x8, starting transfers between devices, collect(): from_left = lax.ppermute(from_left, axis, right)  562 us
    ppermute x8, waiting for transfers between devices, collect(): from_left = lax.ppermute(from_left, axis, right)  366 us
    all_gather x1, waiting for transfers between devices, shards(): lax.all_gather(d_gu_b, 'shard', axis=0, tiled=True)  320 us
    all_gather x1, blocking collectives, shards(): lax.all_gather(q_gain, 'shard', axis=0, tiled=True)  145 us
    psum x1, waiting for transfers between devices, shards(): lax.psum(grad_qkv_own.astype(jnp.bfloat16), 'rep').astype(jnp.float32)  114 us
    all_gather x1, waiting for transfers between devices, shards(): lax.all_gather(d_qkv_b, 'shard', axis=0, tiled=True)  103 us
    dot_general x4, matrix products, contract_last(): lax.dot_general(left, right, (((1,), (1,)), ((), ())), preferred_element_...  73 us
    ppermute x7, waiting for transfers between devices, collect(): from_right = lax.ppermute(from_right, axis, downward)  65.8 us
  transfers between devices with their start and end apart: 27, of which 12 were waited for; matrix products, arithmetic and copies ran while one was open for 12% of the time, Pallas kernels for 0%

profile of v1, /device:TPU:0, one launch (start us, length us, event | category | flops | bytes accessed | tf_op | source)
XLA Modules:
  0.0 2316.6 jit_solution(10462330722076007763)
XLA Ops:
  10.6 5.0 collective-permute-start.1
  15.6 84.3 %collective-permute-done = bf16[128,16384]{1,0:T(8,128)(2,1)S(1)} collective-permute-done((bf16[128,16384]{1,0:T(8,128)(2,1)}, bf16[128,16384]{1,0:T(8,128)(2,1)S(1)}, u32[]{:S(2)}, u32[]{:S(2)}) %collective-permute-start) | collective-permute-done | bytes 4194336 | tf_op jit(solution)/shard_map/ppermute | solution.py:20
  101.9 133.2 %collective-permute-start.2 = (bf16[128,16384]{1,0:T(8,128)(2,1)S(1)}, bf16[128,16384]{1,0:T(8,128)(2,1)}, u32[]{:S(2)}, u32[]{:S(2)}) collective-permute-start(bf16[128,16384]{1,0:T(8,128)(2,1)S(1)} %collective-permute-done), channel_id=1, source_target_pairs={{0,1},{1,2},{2,3},{3,4},{4,5},{5,6},{6,7},{7,8},{8,9},{9,10},{10,1... | collective-permute-start | bytes 12582920 | tf_op jit(solution)/shard_map/ppermute | solution.py:20
  235.1 7.5 collective-permute-done.2
  242.6 114.0 %collective-permute-start.4 = (bf16[128,16384]{1,0:T(8,128)(2,1)}, bf16[128,16384]{1,0:T(8,128)(2,1)}, u32[]{:S(2)}, u32[]{:S(2)}) collective-permute-start(bf16[128,16384]{1,0:T(8,128)(2,1)} %collective-permute-done.2), channel_id=1, source_target_pairs={{0,1},{1,2},{2,3},{3,4},{4,5},{5,6},{6,7},{7,8},{8,9},{9,10},{10,1... | collective-permute-start | bytes 12582920 | tf_op jit(solution)/shard_map/ppermute | solution.py:20
  357.3 21.7 broadcast_in_dim.27
  381.3 29.2 %collective-permute-start.6 = (bf16[128,16384]{1,0:T(8,128)(2,1)}, bf16[128,16384]{1,0:T(8,128)(2,1)}, u32[]{:S(2)}, u32[]{:S(2)}) collective-permute-start(bf16[128,16384]{1,0:T(8,128)(2,1)} %collective-permute-done.4), channel_id=1, source_target_pairs={{0,1},{1,2},{2,3},{3,4},{4,5},{5,6},{6,7},{7,8},{8,9},{9,10},{10,1... | collective-permute-start | bytes 12582920 | tf_op jit(solution)/shard_map/ppermute | solution.py:20
  410.6 145.0 %all-gather = bf16[16,1,128]{2,1,0:T(2,128)(2,1)S(1)} all-gather(bf16[1,1,128]{2,1,0:T(2,128)(2,1)S(1)} %bitcast.143), channel_id=1, replica_groups=mesh['rep'=2,'shard'=16] {'shard'}, dimensions={0}, use_global_device_ids=true | all-gather | bytes 4352 | tf_op jit(solution)/shard_map/all_gather | solution.py:205
  555.6 18.6 all-gather.1
  574.2 18.5 all-gather.2
  592.7 18.8 all-gather.3
  611.9 4.8 constant_dynamic-update-slice_fusion.14
  617.4 4.8 constant_dynamic-update-slice_fusion.13
  626.8 4.7 constant_dynamic-update-slice_fusion.11
  631.4 65.8 %collective-permute-done.7 = bf16[128,16384]{1,0:T(8,128)(2,1)S(1)} collective-permute-done((bf16[128,16384]{1,0:T(8,128)(2,1)}, bf16[128,16384]{1,0:T(8,128)(2,1)S(1)}, u32[]{:S(2)}, u32[]{:S(2)}) %collective-permute-start.7) | collective-permute-done | bytes 4194336 | tf_op jit(solution)/shard_map/ppermute | solution.py:25
  701.8 4.6 constant_dynamic-update-slice_fusion.10
  706.4 6.8 collective-permute-done.8
  713.2 105.7 %collective-permute-start.10 = (bf16[128,16384]{1,0:T(8,128)(2,1)S(1)}, bf16[128,16384]{1,0:T(8,128)(2,1)S(1)}, u32[]{:S(2)}, u32[]{:S(2)}) collective-permute-start(bf16[128,16384]{1,0:T(8,128)(2,1)S(1)} %collective-permute-done.8), channel_id=1, source_target_pairs={{0,1},{1,2},{2,3},{3,4},{4,5},{5,6},{6,7},{7,8},{8,9},{9,10},{10,1... | collective-permute-start | bytes 12582920 | tf_op jit(solution)/shard_map/ppermute | solution.py:20
  830.2 102.3 %collective-permute-done.10 = bf16[128,16384]{1,0:T(8,128)(2,1)S(1)} collective-permute-done((bf16[128,16384]{1,0:T(8,128)(2,1)S(1)}, bf16[128,16384]{1,0:T(8,128)(2,1)S(1)}, u32[]{:S(2)}, u32[]{:S(2)}) %collective-permute-start.10) | collective-permute-done | bytes 4194336 | tf_op jit(solution)/shard_map/ppermute | solution.py:20
  932.5 89.6 %collective-permute-start.12 = (bf16[128,16384]{1,0:T(8,128)(2,1)S(1)}, bf16[128,16384]{1,0:T(8,128)(2,1)S(1)}, u32[]{:S(2)}, u32[]{:S(2)}) collective-permute-start(bf16[128,16384]{1,0:T(8,128)(2,1)S(1)} %collective-permute-done.10), channel_id=1, source_target_pairs={{0,1},{1,2},{2,3},{3,4},{4,5},{5,6},{6,7},{7,8},{8,9},{9,10},{10,1... | collective-permute-start | bytes 12582920 | tf_op jit(solution)/shard_map/ppermute | solution.py:20
  1028.9 49.7 %collective-permute-done.12 = bf16[128,16384]{1,0:T(8,128)(2,1)S(1)} collective-permute-done((bf16[128,16384]{1,0:T(8,128)(2,1)S(1)}, bf16[128,16384]{1,0:T(8,128)(2,1)S(1)}, u32[]{:S(2)}, u32[]{:S(2)}) %collective-permute-start.12) | collective-permute-done | bytes 4194336 | tf_op jit(solution)/shard_map/ppermute | solution.py:20
  1078.6 89.3 %collective-permute-start.14 = (bf16[128,16384]{1,0:T(8,128)(2,1)S(1)}, bf16[128,16384]{1,0:T(8,128)(2,1)S(1)}, u32[]{:S(2)}, u32[]{:S(2)}) collective-permute-start(bf16[128,16384]{1,0:T(8,128)(2,1)S(1)} %collective-permute-done.12), channel_id=1, source_target_pairs={{0,1},{1,2},{2,3},{3,4},{4,5},{5,6},{6,7},{7,8},{8,9},{9,10},{10,1... | collective-permute-start | bytes 12582920 | tf_op jit(solution)/shard_map/ppermute | solution.py:20
  1174.9 115.7 %collective-permute-done.14 = bf16[128,16384]{1,0:T(8,128)(2,1)S(1)} collective-permute-done((bf16[128,16384]{1,0:T(8,128)(2,1)S(1)}, bf16[128,16384]{1,0:T(8,128)(2,1)S(1)}, u32[]{:S(2)}, u32[]{:S(2)}) %collective-permute-start.14) | collective-permute-done | bytes 4194336 | tf_op jit(solution)/shard_map/ppermute | solution.py:20
  1292.8 10.3 fusion.27
  1310.2 5.3 multiply_reduce_fusion.8
  1317.5 27.9 %fusion.28 = f32[128,16384]{1,0:T(8,128)} fusion(bf16[128,2048]{1,0:T(8,128)(2,1)} %fusion.10, bf16[2048,16384]{1,0:T(8,128)(2,1)} %constant_dynamic-update-slice_fusion), kind=kOutput, calls=%fused_computation.121 | convolution fusion | flops 8589934592 | bytes 76021760 | tf_op jit(solution)/shard_map/dot_general | solution.py:159
  1345.4 6.1 multiply_convert_fusion.2
  1351.5 14.0 multiply_reduce_fusion.7
  1367.7 20.1 multiply_convert_fusion.1
  1387.8 31.0 %multiply_reduce_fusion.1 = (bf16[2048]{0:T(1024)(128)(2,1)S(1)}, f32[128]{0:T(128)S(1)}, f32[128,2048]{1,0:T(8,128)}) fusion(f32[128,2048]{1,0:T(8,128)} %copy-done.2, f32[128]{0:T(128)S(1)} %add_rsqrt_fusion.1, f32[2048]{0:T(1024)S(1)} %bitcast.131, bf16[2048,16384]{1,0:T(8,128)(2,1)} %all-gather.19.cloned.1.call-done, ...), kind=kOutput, calls=%fused_computation.36 | convolution fusion | flops 8600680448 | bytes 73938432 | tf_op jit(solution)/shard_map/dot_general | solution.py:85
  1422.5 7.3 convolution_convert_fusion.4
  1451.5 62.4 %all_to_all.73 = bf16[128,16,128]{0,2,1:T(8,128)(2,1)} all-to-all(bf16[128,16,128]{0,2,1:T(8,128)(2,1)S(1)} %bitcast.127), channel_id=1, replica_groups=mesh['rep'=2,'shard'=16] {'shard'}, dimensions={1} | all-to-all | bytes 1048576 | tf_op jit(solution)/shard_map/all_to_all | solution.py:270
  1513.9 7.1 all-to-all-start.1
  1522.5 21.3 all-to-all-done.1
  1543.8 9.9 all-to-all-start.3
  1555.2 52.3 %all-to-all-done.3 = bf16[128,16,512]{2,0,1:T(8,128)(2,1)} async-done(((bf16[128,16,512]{2,0,1:T(8,128)(2,1)}), bf16[128,16,512]{2,0,1:T(8,128)(2,1)}, u32[]{:S(2)}, u32[]{:S(2)}) %all-to-all-start.3) | async-done | bytes 2097184 | tf_op jit(solution)/shard_map/all_to_all | solution.py:268
  1607.6 13.6 all-to-all-start.2
  1621.5 10.0 convolution_convert_fusion.2
  1631.5 5.5 convolution_convert_fusion.3
  1636.9 102.7 %all-gather.21.cloned.1.call-done = bf16[2048,6144]{1,0:T(8,128)(2,1)} async-done(((bf16[128,6144]{1,0:T(8,128)(2,1)}), bf16[2048,6144]{1,0:T(8,128)(2,1)}) %all-gather.21.cloned.1.call-update) | async-done | bytes 25165840 | tf_op jit(solution)/shard_map/all_gather | solution.py:278
  1739.6 13.1 fusion
  1752.8 320.0 %all-gather.25.cloned.1.call-done = bf16[2048,16384]{1,0:T(8,128)(2,1)} async-done(((bf16[128,16384]{1,0:T(8,128)(2,1)}), bf16[2048,16384]{1,0:T(8,128)(2,1)}) %all-gather.25.cloned.1.call-update) | async-done | bytes 67108880 | tf_op jit(solution)/shard_map/all_gather | solution.py:277
  2072.8 26.2 %convolution_convert_fusion = bf16[128,16384]{1,0:T(8,128)(2,1)} fusion(bf16[2048,128]{1,0:T(8,128)(2,1)S(1)} %bitcast.124, bf16[2048,16384]{1,0:T(8,128)(2,1)} %all-gather.25.cloned.1.call-done), kind=kOutput, calls=%fused_computation | convolution fusion | flops 8592031744 | bytes 71827456 | tf_op jit(solution)/shard_map/dot_general | solution.py:91
  2100.8 60.7 %all-reduce.4 = (bf16[2048]{0:T(1024)(128)(2,1)S(1)}, bf16[2048]{0:T(1024)(128)(2,1)S(1)}, bf16[2048]{0:T(1024)(128)(2,1)S(1)}, bf16[2048]{0:T(1024)(128)(2,1)S(1)}) all-reduce(bf16[2048]{0:T(1024)(128)(2,1)S(1)} %get-tuple-element.55, ...), channel_id=2, replica_groups=mesh['rep'=2,'shard'=16] {'shard'}, use_global_device_ids=true, to_apply=%region_17.18.clone | all-reduce | flops 8192 | bytes 32768
  2161.8 5.1 all-reduce.5
  2169.0 14.7 convolution_add_fusion
  2183.7 113.6 %all-reduce.9.cloned.1.call-done = (bf16[128,6144]{0,1:T(8,128)(2,1)}, bf16[128,2048]{1,0:T(8,128)(2,1)}, bf16[128,16384]{1,0:T(8,128)(2,1)}, bf16[512,2048]{1,0:T(8,128)(2,1)}) async-done(((bf16[128,6144]{0,1:T(8,128)(2,1)}, bf16[128,2048]{1,0:T(8,128)(2,1)}, bf16[128,16384]{1,0:T(8,128)(2,1)}, bf16[512,2048]{1,0:T(8,128)(2,1)}), (bf16[128,6144]{0,1:T(8,128)(2,1)}, bf16[128,2048]{1,0:T(8,128)(2,1)}, ...) | async-done | bytes 8388624 | tf_op jit(solution)/shard_map/psum | solution.py:297
  2297.3 6.6 convert_element_type.154
  (190 shorter events, 94.8 us)
Async XLA Ops:
  7.2 349.4 %copy-start.30 = (s32[128]{0:T(128)S(1)}, s32[128]{0:T(128)}, u32[]{:S(2)}) copy-start(s32[128]{0:T(128)} %param.12) | copy-start | bytes 1540
  7.2 1285.6 %all-gather.13.cloned.1.call-start = ((), (), s32[]{:S(2)}) async-start(), calls=%async_computation.4 | async-start | bytes 26738688 | tf_op jit(solution)/shard_map/all_gather | solution.py:204
  7.9 1302.2 %all-gather.15.cloned.1.call-start = ((), (), s32[]{:S(2)}) async-start(), calls=%async_computation.5 | async-start | bytes 8912896 | tf_op jit(solution)/shard_map/all_gather | solution.py:221
  8.7 1342.9 %all-gather.17.cloned.1.call-start = ((), (), s32[]{:S(2)}) async-start(), calls=%async_computation.6 | async-start | bytes 35651584 | tf_op jit(solution)/shard_map/all_gather | solution.py:239
  9.4 1378.4 %all-gather.19.cloned.1.call-start = ((), (), s32[]{:S(2)}) async-start(), calls=%async_computation.7 | async-start | bytes 71303168 | tf_op jit(solution)/shard_map/all_gather | solution.py:250
  10.0 1611.5 %all-gather.27.cloned.1.call-start = ((), (), s32[]{:S(2)}) async-start(), calls=%async_computation.11 | async-start | bytes 8912896 | tf_op jit(solution)/shard_map/all_gather | solution.py:276
  10.0 89.9 %collective-permute-start = (bf16[128,16384]{1,0:T(8,128)(2,1)}, bf16[128,16384]{1,0:T(8,128)(2,1)S(1)}, u32[]{:S(2)}, u32[]{:S(2)}) collective-permute-start(bf16[128,16384]{1,0:T(8,128)(2,1)} %param.16), channel_id=1, source_target_pairs={{0,1},{1,2},{2,3},{3,4},{4,5},{5,6},{6,7},{7,8},{8,9},{9,10},{10,1... | collective-permute-start | bytes 12582920 | tf_op jit(solution)/shard_map/ppermute | solution.py:20
  10.6 224.5 %collective-permute-start.1 = (bf16[128,16384]{1,0:T(8,128)(2,1)}, bf16[128,16384]{1,0:T(8,128)(2,1)}, u32[]{:S(2)}, u32[]{:S(2)}) collective-permute-start(bf16[128,16384]{1,0:T(8,128)(2,1)} %param.16), channel_id=1, source_target_pairs={{0,15},{1,0},{2,1},{3,2},{4,3},{5,4},{6,5},{7,6},{8,7},{9,8},{10,9... | collective-permute-start | bytes 12582920 | tf_op jit(solution)/shard_map/ppermute | solution.py:25
  101.9 140.7 %collective-permute-start.2 = (bf16[128,16384]{1,0:T(8,128)(2,1)S(1)}, bf16[128,16384]{1,0:T(8,128)(2,1)}, u32[]{:S(2)}, u32[]{:S(2)}) collective-permute-start(bf16[128,16384]{1,0:T(8,128)(2,1)S(1)} %collective-permute-done), channel_id=1, source_target_pairs={{0,1},{1,2},{2,3},{3,4},{4,5},{5,6},{6,7},{7,8},{8,9},{9,10},{10,1... | collective-permute-start | bytes 12582920 | tf_op jit(solution)/shard_map/ppermute | solution.py:20
  235.1 122.1 %collective-permute-start.3 = (bf16[128,16384]{1,0:T(8,128)(2,1)}, bf16[128,16384]{1,0:T(8,128)(2,1)}, u32[]{:S(2)}, u32[]{:S(2)}) collective-permute-start(bf16[128,16384]{1,0:T(8,128)(2,1)} %collective-permute-done.1), channel_id=1, source_target_pairs={{0,15},{1,0},{2,1},{3,2},{4,3},{5,4},{6,5},{7,6},{8,7},{9,8},{10,9... | collective-permute-start | bytes 12582920 | tf_op jit(solution)/shard_map/ppermute | solution.py:25
  242.6 138.7 %collective-permute-start.4 = (bf16[128,16384]{1,0:T(8,128)(2,1)}, bf16[128,16384]{1,0:T(8,128)(2,1)}, u32[]{:S(2)}, u32[]{:S(2)}) collective-permute-start(bf16[128,16384]{1,0:T(8,128)(2,1)} %collective-permute-done.2), channel_id=1, source_target_pairs={{0,1},{1,2},{2,3},{3,4},{4,5},{5,6},{6,7},{7,8},{8,9},{9,10},{10,1... | collective-permute-start | bytes 12582920 | tf_op jit(solution)/shard_map/ppermute | solution.py:20
  357.2 21.8 copy-start.3
  357.3 259.4 %collective-permute-start.5 = (bf16[128,16384]{1,0:T(8,128)(2,1)}, bf16[128,16384]{1,0:T(8,128)(2,1)}, u32[]{:S(2)}, u32[]{:S(2)}) collective-permute-start(bf16[128,16384]{1,0:T(8,128)(2,1)} %collective-permute-done.3), channel_id=1, source_target_pairs={{0,15},{1,0},{2,1},{3,2},{4,3},{5,4},{6,5},{7,6},{8,7},{9,8},{10,9... | collective-permute-start | bytes 12582920 | tf_op jit(solution)/shard_map/ppermute | solution.py:25
  379.0 31.5 %copy-start.31 = (bf16[128]{0:T(256)(128)(2,1)S(1)}, bf16[128]{0:T(256)(128)(2,1)}, u32[]{:S(2)}) copy-start(bf16[128]{0:T(256)(128)(2,1)} %param.18) | copy-start | bytes 772
  379.0 176.5 %copy-start.32 = (bf16[128]{0:T(256)(128)(2,1)S(1)}, bf16[128]{0:T(256)(128)(2,1)}, u32[]{:S(2)}) copy-start(bf16[128]{0:T(256)(128)(2,1)} %param.19) | copy-start | bytes 772
  379.0 195.1 %copy-start.33 = (bf16[128]{0:T(256)(128)(2,1)S(1)}, bf16[128]{0:T(256)(128)(2,1)}, u32[]{:S(2)}) copy-start(bf16[128]{0:T(256)(128)(2,1)} %param.20) | copy-start | bytes 772
  379.1 213.6 %copy-start.34 = (bf16[128]{0:T(256)(128)(2,1)S(1)}, bf16[128]{0:T(256)(128)(2,1)}, u32[]{:S(2)}) copy-start(bf16[128]{0:T(256)(128)(2,1)} %param.21) | copy-start | bytes 772
  381.3 240.9 %collective-permute-start.6 = (bf16[128,16384]{1,0:T(8,128)(2,1)}, bf16[128,16384]{1,0:T(8,128)(2,1)}, u32[]{:S(2)}, u32[]{:S(2)}) collective-permute-start(bf16[128,16384]{1,0:T(8,128)(2,1)} %collective-permute-done.4), channel_id=1, source_target_pairs={{0,1},{1,2},{2,3},{3,4},{4,5},{5,6},{6,7},{7,8},{8,9},{9,10},{10,1... | collective-permute-start | bytes 12582920 | tf_op jit(solution)/shard_map/ppermute | solution.py:20
  616.7 80.6 %collective-permute-start.7 = (bf16[128,16384]{1,0:T(8,128)(2,1)}, bf16[128,16384]{1,0:T(8,128)(2,1)S(1)}, u32[]{:S(2)}, u32[]{:S(2)}) collective-permute-start(bf16[128,16384]{1,0:T(8,128)(2,1)} %collective-permute-done.5), channel_id=1, source_target_pairs={{0,15},{1,0},{2,1},{3,2},{4,3},{5,4},{6,5},{7,6},{8,7},{9,8},{10,9... | collective-permute-start | bytes 12582920 | tf_op jit(solution)/shard_map/ppermute | solution.py:25
  622.2 91.0 %collective-permute-start.8 = (bf16[128,16384]{1,0:T(8,128)(2,1)}, bf16[128,16384]{1,0:T(8,128)(2,1)S(1)}, u32[]{:S(2)}, u32[]{:S(2)}) collective-permute-start(bf16[128,16384]{1,0:T(8,128)(2,1)} %collective-permute-done.6), channel_id=1, source_target_pairs={{0,1},{1,2},{2,3},{3,4},{4,5},{5,6},{6,7},{7,8},{8,9},{9,10},{10,1... | collective-permute-start | bytes 12582920 | tf_op jit(solution)/shard_map/ppermute | solution.py:20
  697.2 130.7 %collective-permute-start.9 = (bf16[128,16384]{1,0:T(8,128)(2,1)S(1)}, bf16[128,16384]{1,0:T(8,128)(2,1)S(1)}, u32[]{:S(2)}, u32[]{:S(2)}) collective-permute-start(bf16[128,16384]{1,0:T(8,128)(2,1)S(1)} %collective-permute-done.7), channel_id=1, source_target_pairs={{0,15},{1,0},{2,1},{3,2},{4,3},{5,4},{6,5},{7,6},{8,7},{9,8},{10,9... | collective-permute-start | bytes 12582920 | tf_op jit(solution)/shard_map/ppermute | solution.py:25
  713.2 219.3 %collective-permute-start.10 = (bf16[128,16384]{1,0:T(8,128)(2,1)S(1)}, bf16[128,16384]{1,0:T(8,128)(2,1)S(1)}, u32[]{:S(2)}, u32[]{:S(2)}) collective-permute-start(bf16[128,16384]{1,0:T(8,128)(2,1)S(1)} %collective-permute-done.8), channel_id=1, source_target_pairs={{0,1},{1,2},{2,3},{3,4},{4,5},{5,6},{6,7},{7,8},{8,9},{9,10},{10,1... | collective-permute-start | bytes 12582920 | tf_op jit(solution)/shard_map/ppermute | solution.py:20
  827.9 198.7 %collective-permute-start.11 = (bf16[128,16384]{1,0:T(8,128)(2,1)S(1)}, bf16[128,16384]{1,0:T(8,128)(2,1)S(1)}, u32[]{:S(2)}, u32[]{:S(2)}) collective-permute-start(bf16[128,16384]{1,0:T(8,128)(2,1)S(1)} %collective-permute-done.9), channel_id=1, source_target_pairs={{0,15},{1,0},{2,1},{3,2},{4,3},{5,4},{6,5},{7,6},{8,7},{9,8},{10,9... | collective-permute-start | bytes 12582920 | tf_op jit(solution)/shard_map/ppermute | solution.py:25
  932.5 146.1 %collective-permute-start.12 = (bf16[128,16384]{1,0:T(8,128)(2,1)S(1)}, bf16[128,16384]{1,0:T(8,128)(2,1)S(1)}, u32[]{:S(2)}, u32[]{:S(2)}) collective-permute-start(bf16[128,16384]{1,0:T(8,128)(2,1)S(1)} %collective-permute-done.10), channel_id=1, source_target_pairs={{0,1},{1,2},{2,3},{3,4},{4,5},{5,6},{6,7},{7,8},{8,9},{9,10},{10,1... | collective-permute-start | bytes 12582920 | tf_op jit(solution)/shard_map/ppermute | solution.py:20
  1026.6 145.9 %collective-permute-start.13 = (bf16[128,16384]{1,0:T(8,128)(2,1)S(1)}, bf16[128,16384]{1,0:T(8,128)(2,1)S(1)}, u32[]{:S(2)}, u32[]{:S(2)}) collective-permute-start(bf16[128,16384]{1,0:T(8,128)(2,1)S(1)} %collective-permute-done.11), channel_id=1, source_target_pairs={{0,15},{1,0},{2,1},{3,2},{4,3},{5,4},{6,5},{7,6},{8,7},{9,8},{10,9... | collective-permute-start | bytes 12582920 | tf_op jit(solution)/shard_map/ppermute | solution.py:25
  1078.6 211.9 %collective-permute-start.14 = (bf16[128,16384]{1,0:T(8,128)(2,1)S(1)}, bf16[128,16384]{1,0:T(8,128)(2,1)S(1)}, u32[]{:S(2)}, u32[]{:S(2)}) collective-permute-start(bf16[128,16384]{1,0:T(8,128)(2,1)S(1)} %collective-permute-done.12), channel_id=1, source_target_pairs={{0,1},{1,2},{2,3},{3,4},{4,5},{5,6},{6,7},{7,8},{8,9},{9,10},{10,1... | collective-permute-start | bytes 12582920 | tf_op jit(solution)/shard_map/ppermute | solution.py:20
  1310.2 6.3 copy-start.5
  1351.5 14.0 copy-start.9
  1367.7 263.8 %all-gather.23.cloned.1.call-start = ((), (), s32[]{:S(2)}) async-start(), calls=%async_computation.9 | async-start | bytes 8912896 | tf_op jit(solution)/shard_map/all_gather | solution.py:279
  1422.3 317.4 %all-gather.21.cloned.1.call-start = ((), (), s32[]{:S(2)}) async-start(), calls=%async_computation.8 | async-start | bytes 26738688 | tf_op jit(solution)/shard_map/all_gather | solution.py:278
  1436.5 3.4 copy-start.15
  1436.5 3.5 copy-start.17
  1436.6 3.9 copy-start.11
  1436.6 3.9 copy-start.13
  1446.1 626.7 %all-gather.25.cloned.1.call-start = ((), (), s32[]{:S(2)}) async-start(), calls=%async_computation.10 | async-start | bytes 71303168 | tf_op jit(solution)/shard_map/all_gather | solution.py:277
  1450.1 70.9 %copy-start.1 = (bf16[128,8192]{1,0:T(8,128)(2,1)S(1)}, bf16[128,8192]{1,0:T(8,128)(2,1)}, u32[]{:S(2)}) copy-start(bf16[128,8192]{1,0:T(8,128)(2,1)} %multiply_convert_fusion.2) | copy-start | bytes 6291460
  1513.9 29.9 %all-to-all-start.1 = ((bf16[128,16,128]{0,2,1:T(8,128)(2,1)}), bf16[128,16,128]{0,2,1:T(8,128)(2,1)S(1)}, u32[]{:S(2)}, u32[]{:S(2)}) async-start(bf16[128,16,128]{0,2,1:T(8,128)(2,1)} %get-tuple-element.103), calls=%async_computation.1 | async-start | bytes 1048576 | tf_op jit(solution)/shard_map/all_to_all | solution.py:271
  1521.0 33.0 %copy-start.8 = (bf16[128,2048]{1,0:T(8,128)(2,1)S(1)}, bf16[128,2048]{1,0:T(8,128)(2,1)}, u32[]{:S(2)}) copy-start(bf16[128,2048]{1,0:T(8,128)(2,1)} %fusion.10) | copy-start | bytes 1572868
  1522.5 31.2 %copy-start.21 = (bf16[128,16,128]{0,2,1:T(8,128)(2,1)S(1)}, bf16[128,16,128]{0,2,1:T(8,128)(2,1)}, u32[]{:S(2)}) copy-start(bf16[128,16,128]{0,2,1:T(8,128)(2,1)} %all_to_all.73) | copy-start | bytes 1572868
  1543.8 63.8 %all-to-all-start.3 = ((bf16[128,16,512]{2,0,1:T(8,128)(2,1)}), bf16[128,16,512]{2,0,1:T(8,128)(2,1)}, u32[]{:S(2)}, u32[]{:S(2)}) async-start(bf16[128,16,512]{2,0,1:T(8,128)(2,1)} %bitcast.120), calls=%async_computation.3 | async-start | bytes 4194304 | tf_op jit(solution)/shard_map/all_to_all | solution.py:268
  1607.6 145.2 %all-to-all-start.2 = ((bf16[128,16,128]{2,0,1:T(8,128)(2,1)}), bf16[128,16,128]{2,0,1:T(8,128)(2,1)S(1)}, u32[]{:S(2)}, u32[]{:S(2)}) async-start(bf16[128,16,128]{2,0,1:T(8,128)(2,1)} %copy_bitcast_fusion.1), calls=%async_computation.2 | async-start | bytes 1048576 | tf_op jit(solution)/shard_map/all_to_all | solution.py:269
  1621.2 676.1 %all-reduce.9.cloned.1.call-start = ((), (), s32[]{:S(2)}) async-start(), calls=%async_computation.12 | async-start | bytes 16777216 | tf_op jit(solution)/shard_map/psum | solution.py:297
  2098.9 70.0 %copy-start.18 = (f32[128,2048]{1,0:T(8,128)S(1)}, f32[128,2048]{1,0:T(8,128)}, u32[]{:S(2)}) copy-start(f32[128,2048]{1,0:T(8,128)} %get-tuple-element.109) | copy-start | bytes 3145732
  2098.9 70.0 %copy-start.23 = (bf16[128,2048]{1,0:T(8,128)(2,1)S(1)}, bf16[128,2048]{1,0:T(8,128)(2,1)}, u32[]{:S(2)}) copy-start(bf16[128,2048]{1,0:T(8,128)(2,1)} %copy.132) | copy-start | bytes 1572868
  2098.9 70.0 %copy-start.25 = (bf16[128,2048]{1,0:T(8,128)(2,1)S(1)}, bf16[128,2048]{1,0:T(8,128)(2,1)}, u32[]{:S(2)}) copy-start(bf16[128,2048]{1,0:T(8,128)(2,1)} %copy-done.24) | copy-start | bytes 1572868
  2099.0 70.0 %copy-start.27 = (bf16[128,2048]{1,0:T(8,128)(2,1)S(1)}, bf16[128,2048]{1,0:T(8,128)(2,1)}, u32[]{:S(2)}) copy-start(bf16[128,2048]{1,0:T(8,128)(2,1)} %copy-done.26) | copy-start | bytes 1572868
  2297.3 6.6 copy-start.20
  2303.9 4.6 copy-start.29
  (15 other events, 20.7 us)
Sparse Core Ops, SparseCore 0:
  9.6 332.8 all-gather.12
  344.6 128.5 all-gather.14
  474.8 273.9 all-gather.16
  750.3 597.2 all-gather.18
  1367.8 108.9 all-gather.26
  1478.8 122.7 all-gather.22
  1603.8 135.7 all-gather.20
  1741.8 330.9 all-gather.24
  2099.1 198.1 all-reduce.8
